TPU v7x, 32 devices: a 4x4x1 block of a 4x4x8 slice. The times are simulated.
32 devices in a mesh: dp: 1 (over z), tp: 32 (over y, x, core).
Axes of the slice: x: 4, y: 4, z: 1, core: 2. Of those that a mesh axis runs over, the one named last changes fastest.
The devices are a block of a 4x4x8 slice.
Arguments:
- hid_one: bfloat16 [256, 9, 2048], P('dp')
- q_one: float32 [256, 8, 32000], P(('dp', 'tp'))
- tok_one: int32 [256, 8], P('dp')
- hid_two: bfloat16 [256, 9, 2048], P('dp')
- q_two: float32 [256, 8, 32000], P(('dp', 'tp'))
- tok_two: int32 [256, 8], P('dp')
- w_head: bfloat16 [2048, 32000], P(None, 'tp')
Outputs:
- output 1: float32 [256, 8], P('dp')
- output 2: float32 [256], P('dp')
- output 3: float32 [256, 8, 32000], P('dp', None, 'tp')
- output 4: float32 [256, 32000], P('dp', 'tp')
- output 5: float32 [256, 8], P('dp')
- output 6: float32 [256], P('dp')
- output 7: float32 [256, 8, 32000], P('dp', None, 'tp')
- output 8: float32 [256, 32000], P('dp', 'tp')
All inputs are finite; a program needn't handle non-finite values.
Results may differ from a plain program's by a relative error of at most 0.001.
Values are sent between devices in bfloat16 or wider.
A program may use at most 768 MiB of HBM per device.

v0:
```python
import jax
import jax.numpy as jnp
from jax import lax
from jax.sharding import PartitionSpec as P

INV_TEMP = 1.25


def verify_local(hidden, q_rows, tokens, w_local):
    vocab_loc = w_local.shape[1]
    offset = lax.axis_index('tp') * vocab_loc
    logits = jnp.einsum('bgd,dv->bgv', hidden, w_local, preferred_element_type=jnp.float32) * INV_TEMP
    row_max = lax.pmax(jnp.max(logits, axis=-1, keepdims=True), 'tp')
    exp_val = jnp.exp(logits - row_max)
    exp_sum = lax.psum(jnp.sum(exp_val, axis=-1, keepdims=True), 'tp')
    prob_all = exp_val / exp_sum
    p_draft = prob_all[:, :-1]
    q_cols = lax.all_to_all(q_rows, 'tp', 2, 0, tiled=True)
    local_tok = tokens - offset
    in_shard = (local_tok >= 0) & (local_tok < vocab_loc)
    tok_clip = jnp.clip(local_tok, 0, vocab_loc - 1)[:, :, None]
    p_pick = jnp.take_along_axis(p_draft, tok_clip, axis=-1)[:, :, 0]
    q_pick = jnp.take_along_axis(q_cols, tok_clip, axis=-1)[:, :, 0]
    pick_pair = lax.psum(jnp.where(in_shard, jnp.stack([p_pick, q_pick]), 0.0), 'tp')
    accept = jnp.minimum(pick_pair[0] / pick_pair[1], 1.0)
    expect = jnp.sum(jnp.cumprod(accept, axis=1), axis=1)
    excess = jnp.maximum(p_draft - q_cols, 0.0)
    resid_sum = lax.psum(jnp.sum(excess, axis=-1, keepdims=True), 'tp')
    return accept, expect, excess / resid_sum, prob_all[:, -1]


def solution(mesh):
    row_spec = P('dp')
    q_spec = P(('dp', 'tp'))
    w_spec = P(None, 'tp')
    vocab_spec = P('dp', None, 'tp')
    value_a10 = P('dp', 'tp')

    def verify_both(hid_one, q_one, tok_one, hid_two, q_two, tok_two, w_local):
        out_one = verify_local(hid_one, q_one, tok_one, w_local)
        out_two = verify_local(hid_two, q_two, tok_two, w_local)
        return out_one + out_two

    out_specs = (row_spec, row_spec, vocab_spec, value_a10, row_spec, row_spec, vocab_spec, value_a10)
    in_specs = (row_spec, q_spec, row_spec, row_spec, q_spec, row_spec, w_spec)
    return jax.shard_map(verify_both, mesh=mesh, in_specs=in_specs, out_specs=out_specs, check_vma=False)
```

profile of v0, /device:TPU:97, one launch (start us, length us, event | category | flops | bytes accessed | tf_op | source)
XLA Modules:
  0.0 1209.2 jit_solution(8378566787338455503)
XLA Ops:
  0.6 58.8 %copy.80 = f32[8,8,32000]{1,0,2:T(8,128)} copy(f32[8,8,32000]{2,1,0:T(8,128)} %param.13) | data formatting | bytes 16384000 | tf_op args[4]
  59.4 74.4 %reshape.110 = f32[32,1,64000]{2,1,0:T(1,128)} reshape(f32[32000,8,8]{2,1,0:T(8,128)} %bitcast.59) | data formatting | bytes 16384000
  133.8 9.1 all-to-all-start.1
  143.0 58.8 %copy.73 = f32[8,8,32000]{1,0,2:T(8,128)} copy(f32[8,8,32000]{2,1,0:T(8,128)} %param.10) | data formatting | bytes 16384000 | tf_op args[1]
  201.8 74.4 %reshape.108 = f32[32,1,64000]{2,1,0:T(1,128)} reshape(f32[32000,8,8]{2,1,0:T(8,128)} %bitcast.57) | data formatting | bytes 16384000
  276.2 15.0 %multiply_reduce_fusion.1 = (f32[256,9]{0,1:T(8,128)S(1)}, f32[256,9,1000]{0,2,1:T(8,128)}) fusion(bf16[256,9,2048]{2,0,1:T(8,128)(2,1)} %param.9, bf16[2048,1000]{0,1:T(8,128)(2,1)} %param.15), kind=kOutput, calls=%fused_computation.7 | convolution fusion | flops 9441789952 | bytes 22758400 | tf_op jit(solution)/shard_map/bgd,dv->bgv/dot_general | solution.py:12
  291.2 6.9 all-to-all-start
  298.1 0.1 copy.78
  298.3 0.1 reshape.97
  298.4 0.1 copy.71
  298.5 0.7 reshape.85
  299.2 14.9 %multiply_reduce_fusion = (f32[256,9]{0,1:T(8,128)S(1)}, f32[256,9,1000]{0,2,1:T(8,128)}) fusion(bf16[256,9,2048]{2,0,1:T(8,128)(2,1)} %param.12, bf16[2048,1000]{0,1:T(8,128)(2,1)} %param.15), kind=kOutput, calls=%fused_computation.6 | convolution fusion | flops 9441789952 | bytes 22758400 | tf_op jit(solution)/shard_map/bgd,dv->bgv/dot_general | solution.py:12
  314.2 129.3 %all-reduce.2 = (f32[256,9]{0,1:T(8,128)S(1)}, f32[256,9]{0,1:T(8,128)S(1)}) all-reduce(f32[256,9]{0,1:T(8,128)S(1)} %get-tuple-element.43, f32[256,9]{0,1:T(8,128)S(1)} %get-tuple-element.45), channel_id=1, replica_groups=mesh['dp'=1,'tp'=32] {'tp'}, use_global_device_ids=true, to_apply=%region_1.0 | all-reduce | flops 4608 | bytes 36864 | tf_op jit(solution)/shard_map/pmax | solution.py:13
  443.5 5.3 fusion.1
  448.8 0.9 copy-done.3
  449.7 1.5 fusion.3
  451.2 45.0 %all-reduce.1 = (f32[256,9]{0,1:T(8,128)S(1)}, f32[256,9]{0,1:T(8,128)S(1)}) all-reduce(f32[256,9]{0,1:T(8,128)S(1)} %fusion.1, f32[256,9]{0,1:T(8,128)S(1)} %fusion.3), channel_id=1, replica_groups=mesh['dp'=1,'tp'=32] {'tp'}, use_global_device_ids=true, to_apply=%region_3.0 | all-reduce | flops 4608 | bytes 36864 | tf_op jit(solution)/shard_map/psum | solution.py:15
  496.2 0.6 compare_and_fusion.2
  496.8 7.8 fusion
  504.6 3.5 copy-done.2
  508.2 1.8 slice_bitcast_fusion
  510.0 1.2 copy-done.1
  511.2 1.0 slice_bitcast_fusion.1
  512.2 0.5 broadcast.185
  512.8 24.8 %reduce.1 = f32[32,64000]{1,0:T(8,128)} reduce(f32[32,1,64000]{2,1,0:T(1,128)} %all-to-all-done.1, f32[]{:T(128)} %broadcast.185), dimensions={1}, to_apply=%all_to_all.30.reduce_sub_computation | reduce | bytes 16384004 | tf_op jit(solution)/shard_map/all_to_all | solution.py:18
  537.5 120.6 %reshape.111 = f32[32000,8,8]{2,1,0:T(8,128)} reshape(f32[32,64000]{1,0:T(8,128)} %reduce.1) | data formatting | bytes 16384000
  658.1 73.0 %copy.81 = f32[8,8,32,1000]{3,1,0,2:T(8,128)} copy(f32[8,8,32,1000]{1,0,3,2:T(8,128)} %bitcast.18) | data formatting | bytes 16384000 | tf_op jit(solution)/shard_map/all_to_all | solution.py:18
  731.2 9.1 copy.84
  740.3 33.7 %gather_fusion.3 = f32[2048]{0:T(1024)S(1)} fusion(f32[256,8,1000]{2,1,0:T(8,128)} %bitcast.72, s32[2048]{0:T(1024)S(1)} %reshape.97), kind=kCustom, calls=%fused_computation.3.clone | custom fusion | bytes 40960 | tf_op jit(solution)/shard_map/jit(take_along_axis)/gather | solution.py:23
  774.0 10.9 fusion.9
  784.8 34.0 %gather_fusion.2 = f32[2048]{0:T(1024)S(1)} fusion(f32[256,8,1000]{0,2,1:T(8,128)} %get-tuple-element.38, s32[2048]{0:T(1024)S(1)} %reshape.97), kind=kCustom, calls=%fused_computation.2.clone | custom fusion | bytes 40960 | tf_op jit(solution)/shard_map/jit(take_along_axis)/gather | solution.py:22
  818.9 0.1 reshape.100
  819.0 0.1 reshape.106
  819.2 0.7 copy.83
  819.8 0.6 select_bitcast_fusion.1
  820.4 24.8 %reduce = f32[32,64000]{1,0:T(8,128)} reduce(f32[32,1,64000]{2,1,0:T(1,128)} %all-to-all-done, f32[]{:T(128)} %broadcast.185), dimensions={1}, to_apply=%all_to_all.26.reduce_sub_computation | reduce | bytes 16384004 | tf_op jit(solution)/shard_map/all_to_all | solution.py:18
  845.2 120.2 %reshape.109 = f32[32000,8,8]{2,1,0:T(8,128)} reshape(f32[32,64000]{1,0:T(8,128)} %reduce) | data formatting | bytes 16384000
  965.4 73.1 %copy.74 = f32[8,8,32,1000]{3,1,0,2:T(8,128)} copy(f32[8,8,32,1000]{1,0,3,2:T(8,128)} %bitcast.5) | data formatting | bytes 16384000 | tf_op jit(solution)/shard_map/all_to_all | solution.py:18
  1038.5 9.1 copy.77
  1047.6 10.3 fusion.8
  1057.9 33.8 %gather_fusion.1 = f32[2048]{0:T(1024)S(1)} fusion(f32[256,8,1000]{2,1,0:T(8,128)} %bitcast.70, s32[2048]{0:T(1024)S(1)} %copy-done), kind=kCustom, calls=%fused_computation.1.clone | custom fusion | bytes 40960 | tf_op jit(solution)/shard_map/jit(take_along_axis)/gather | solution.py:23
  1091.8 34.2 %gather_fusion = f32[2048]{0:T(1024)S(1)} fusion(f32[256,8,1000]{0,2,1:T(8,128)} %get-tuple-element.40, s32[2048]{0:T(1024)S(1)} %copy-done), kind=kCustom, calls=%fused_computation.clone | custom fusion | bytes 40960 | tf_op jit(solution)/shard_map/jit(take_along_axis)/gather | solution.py:22
  1126.0 0.1 reshape.88
  1126.5 62.1 %all-reduce = (f32[2,256,8]{1,2,0:T(8,128)S(1)}, f32[256,8]{0,1:T(8,128)S(1)}, f32[2,256,8]{1,2,0:T(8,128)S(1)}, f32[256,8]{0,1:T(8,128)S(1)}) all-reduce(f32[2,256,8]{1,2,0:T(8,128)S(1)} %maximum_select_fusion, f32[256,8]{0,1:T(8,128)S(1)} %get-tuple-element.39, ...), channel_id=1, replica_groups=mesh['dp'=1,'tp'=32] {'tp'}, use_global_device_ids=true, to_apply=%region_4.0 | all-reduce | flops 12288 | bytes 98304 | tf_op jit(solution)/shard_map/psum | solution.py:24
  1188.5 9.6 broadcast_divide_fusion
  1198.1 9.6 broadcast_divide_fusion.1
  1207.8 0.6 reduce_sum.55
  1208.4 0.6 reduce_sum.58
  (50 shorter events, 0.5 us)
Async XLA Ops:
  133.8 157.4 %all-to-all-start.1 = ((f32[32,1,64000]{2,1,0:T(1,128)}), f32[32,1,64000]{2,1,0:T(1,128)}, u32[]{:S(2)}, u32[]{:S(2)}) async-start(f32[32,1,64000]{2,1,0:T(1,128)} %reshape.110), calls=%async_computation.1 | async-start | bytes 16384000 | tf_op jit(solution)/shard_map/all_to_all | solution.py:18
  201.8 74.4 %copy-start.4 = (s32[256,8]{0,1:T(8,128)S(1)}, s32[256,8]{0,1:T(8,128)}, u32[]{:S(2)}) copy-start(s32[256,8]{0,1:T(8,128)} %param.14) | copy-start | bytes 24580
  201.8 74.4 %copy-start.6 = (s32[256,8]{0,1:T(8,128)S(1)}, s32[256,8]{0,1:T(8,128)}, u32[]{:S(2)}) copy-start(s32[256,8]{0,1:T(8,128)} %param.11) | copy-start | bytes 24580
  291.2 529.2 %all-to-all-start = ((f32[32,1,64000]{2,1,0:T(1,128)}), f32[32,1,64000]{2,1,0:T(1,128)}, u32[]{:S(2)}, u32[]{:S(2)}) async-start(f32[32,1,64000]{2,1,0:T(1,128)} %reshape.108), calls=%async_computation | async-start | bytes 16384000 | tf_op jit(solution)/shard_map/all_to_all | solution.py:18
  443.5 6.2 copy-start.3
  504.6 3.6 copy-start.2
  504.6 6.6 copy-start.1
  784.8 35.0 %copy-start.5 = (s32[256,8]{0,1:T(8,128)S(1)}, s32[256,8]{0,1:T(8,128)}, u32[]{:S(2)}) copy-start(s32[256,8]{0,1:T(8,128)} %param.14) | copy-start | bytes 24580
  1047.6 10.3 copy-start
  1091.7 34.4 %copy-start.7 = (s32[256,8]{0,1:T(8,128)S(1)}, s32[256,8]{0,1:T(8,128)}, u32[]{:S(2)}) copy-start(s32[256,8]{0,1:T(8,128)} %param.11) | copy-start | bytes 24580
  1091.7 34.6 %copy-start.10 = (f32[256,8,1]{0,1,2:T(8,128)S(1)}, f32[256,8,1]{0,1,2:T(8,128)}, u32[]{:S(2)}) copy-start(f32[256,8,1]{0,1,2:T(8,128)} %copy.83) | copy-start | bytes 24580
  1091.8 34.6 %copy-start.15 = (pred[256,8,1]{0,1,2:T(8,128)(4,1)S(1)}, pred[256,8,1]{0,1,2:T(8,128)(4,1)}, u32[]{:S(2)}) copy-start(pred[256,8,1]{0,1,2:T(8,128)(4,1)} %get-tuple-element.34) | copy-start | bytes 6148
  1091.8 34.6 %copy-start.9 = (f32[1,256,8]{1,2,0:T(8,128)S(1)}, f32[1,256,8]{1,2,0:T(8,128)}, u32[]{:S(2)}) copy-start(f32[1,256,8]{1,2,0:T(8,128)} %get-tuple-element.33) | copy-start | bytes 24580
  1091.8 34.6 %copy-start.14 = (pred[256,8]{0,1:T(8,128)(4,1)S(1)}, pred[256,8]{0,1:T(8,128)(4,1)}, u32[]{:S(2)}) copy-start(pred[256,8]{0,1:T(8,128)(4,1)} %get-tuple-element.49) | copy-start | bytes 6148
  1091.8 34.6 %copy-start.13 = (pred[256,8]{0,1:T(8,128)(4,1)S(1)}, pred[256,8]{0,1:T(8,128)(4,1)}, u32[]{:S(2)}) copy-start(pred[256,8]{0,1:T(8,128)(4,1)} %get-tuple-element.50) | copy-start | bytes 6148
  1091.8 34.6 %copy-start.8 = (f32[256,8]{0,1:T(8,128)S(1)}, f32[256,8]{0,1:T(8,128)}, u32[]{:S(2)}) copy-start(f32[256,8]{0,1:T(8,128)} %get-tuple-element.37) | copy-start | bytes 24580
  1207.8 1.2 copy-start.11
  1207.8 1.2 copy-start.12
where the time goes:
time: 1230 us; the launch traced here: 1210 us
  local copies, waits for them, and re-layouts  819 us (67%)
  blocking collectives  236 us (19%)
  other arithmetic  107 us (9%)
  matrix products  29.9 us (2%)
  starting transfers between devices  16.1 us (1%)
    unnamed x38, local copies, waits for them, and re-layouts  513 us
    all_to_all x5, local copies, waits for them, and re-layouts, verify_local(): q_cols = lax.all_to_all(q_rows, 'tp', 2, 0, tiled=True)  165 us
    pmax x1, blocking collectives, verify_local(): row_max = lax.pmax(jnp.max(logits, axis=-1, keepdims=True), 'tp')  129 us
    gather x10, local copies, waits for them, and re-layouts, verify_local(): p_pick = jnp.take_along_axis(p_draft, tok_clip, axis=-1)[:, :, 0]  69.6 us
    gather x6, local copies, waits for them, and re-layouts, verify_local(): q_pick = jnp.take_along_axis(q_cols, tok_clip, axis=-1)[:, :, 0]  68.4 us
    psum x1, blocking collectives, verify_local(): lax.psum(jnp.where(in_shard, jnp.stack([p_pick, q_pick]), 0.0), 'tp')  62.1 us
    all_to_all x2, other arithmetic, verify_local(): q_cols = lax.all_to_all(q_rows, 'tp', 2, 0, tiled=True)  49.6 us
    psum x1, blocking collectives, verify_local(): exp_sum = lax.psum(jnp.sum(exp_val, axis=-1, keepdims=True), 'tp')  45 us
  transfers between devices with their start and end apart: 2, of which 0 were waited for; matrix products, arithmetic and copies ran while one was open for 41% of the time, Pallas kernels for 0%

commit v1 on v0

v1 whole, which is shorter than its diff:
```python
import functools
import math

import jax
import jax.numpy as jnp
from jax import lax
from jax.experimental import pallas as pl
from jax.experimental.pallas import tpu as pltpu
from jax.sharding import PartitionSpec as P

INV_TEMP = 1.25
LANES = 128
SUBLANES = 8
SLOTS = 8
HEAD_ROUNDS = 4
COL_TILE = 256
MESH = pl.DeviceIdType.MESH


def partner_steps(n):
    side = math.isqrt(n // 2)
    groups = {}
    for dy in range(side):
        for dx in range(side):
            hops = tuple(sorted((min(dy, side - dy), min(dx, side - dx)), reverse=True))
            groups.setdefault(hops, []).append((dy, dx))
    order = [(2, 2), (2, 1), (2, 0), (1, 0), (1, 1), (0, 0)]
    order += [k for k in groups if k not in order]
    steps = []
    for key in order:
        for dc in range(2):
            for dy, dx in groups.get(key, []):
                if (dy, dx, dc) != (0, 0, 0):
                    steps.append((dy, dx, dc))
    return steps


def exchange_kernel(n, hid_one, hid_two, q_one, q_two, tok_one, tok_two, w_hbm,
                    ex, eb, fin,
                    w_buf, hid_buf, q_buf, stage, recv, loc_max, tok_buf,
                    st_send, st_recv, st_out, st_res, z_send, z_recv, z_out, z_res,
                    q_sem, w_sem, hid_sem, send_sem, recv_sem, st_sem, z_sem):
    me = lax.axis_index('tp')
    depth, batch = tok_one.shape
    vocab = w_hbm.shape[0]
    halves = batch // LANES
    rounds = 2 * depth
    hids, qs, toks = (hid_one, hid_two), (q_one, q_two), (tok_one, tok_two)
    side = math.isqrt(n // 2)
    core, chip = lax.rem(me, 2), me // 2
    col, row = lax.rem(chip, side), chip // side
    steps = partner_steps(n)

    def partner(step):
        dy, dx, dc = step
        return (lax.rem(row + dy, side) * side + lax.rem(col + dx, side)) * 2 + lax.rem(core + dc, 2)

    barrier = pltpu.get_barrier_semaphore()
    for step in steps:
        pl.semaphore_signal(barrier, inc=1, device_id={'tp': partner(step)}, device_id_type=MESH)

    q_tiles = q_one.shape[1] // LANES

    def load_q(mb):
        def one(t, carry):
            cols = pl.ds(pl.multiple_of(t * LANES, LANES), LANES)
            pltpu.make_async_copy(qs[mb].at[:, cols], q_buf.at[t], q_sem).start()
            return carry

        lax.fori_loop(0, q_tiles, one, 0)

    def wait_q():
        block = q_buf.at[pl.ds(0, q_tiles)]
        pltpu.make_async_copy(block, block, q_sem).wait()

    def load_hid(mb, i, slot):
        return pltpu.make_async_copy(hids[mb].at[i], hid_buf.at[slot], hid_sem.at[slot])

    load_q(0)
    load_w = pltpu.make_async_copy(w_hbm, w_buf, w_sem)
    load_w.start()
    load_hid(0, 0, 0).start()
    st_send[...] = jnp.zeros_like(st_send)
    z_send[...] = jnp.zeros_like(z_send)
    st_out[...] = jnp.zeros_like(st_out)
    z_out[...] = jnp.zeros_like(z_out)
    for g in range(rounds):
        i = g % depth
        tok_buf[g] = toks[g // depth][i:i + 1, :]
    lane = lax.broadcasted_iota(jnp.int32, (SUBLANES, LANES), 1)
    tiles = pl.cdiv(vocab, LANES)

    def pack(r):
        i, slot = lax.rem(r, depth), lax.rem(r, SLOTS)

        def one(d, carry):
            start = d * vocab
            base, off = start // LANES, lax.rem(start, LANES)
            shift = lax.rem(LANES - off, LANES)
            rolled = []
            for t in range(tiles + 1):
                rolled.append(pltpu.roll(q_buf[base + t, pl.ds(i, SUBLANES, stride=depth), :], shift, 1))
            for t in range(tiles):
                stage[slot, d, :, t * LANES:(t + 1) * LANES] = jnp.where(lane < LANES - off, rolled[t], rolled[t + 1])
            return carry

        lax.fori_loop(0, n, one, 0)

    def send(r):
        slot = lax.rem(r, SLOTS)
        mine = pl.ds(pl.multiple_of(me * SUBLANES, SUBLANES), SUBLANES)
        for step in steps:
            to = partner(step)
            pltpu.make_async_remote_copy(
                src_ref=stage.at[slot, to], dst_ref=recv.at[r, mine],
                send_sem=send_sem.at[slot], recv_sem=recv_sem.at[r],
                device_id={'tp': to}, device_id_type=MESH).start()
        recv[r, mine, :] = stage[slot, me]

    def wait_send(r):
        block = stage.at[lax.rem(r, SLOTS), pl.ds(0, n - 1)]
        pltpu.make_async_copy(block, block, send_sem.at[lax.rem(r, SLOTS)]).wait()

    def wait_tiles(ref, sem):
        block = ref.at[pl.ds(0, n - 1)]
        pltpu.make_async_copy(block, block, sem).wait()

    wait_q()
    pack(0)
    pl.semaphore_wait(barrier, n - 1)
    send(0)

    def head_round(r, carry):
        pack(r)
        send(r)
        return carry

    lax.fori_loop(1, HEAD_ROUNDS, head_round, 0)

    load_w.wait()
    spans = [(v, min(COL_TILE, vocab - v)) for v in range(0, vocab, COL_TILE)]

    def logits(hid_slot, out):
        top = None
        for v, size in spans:
            z = lax.dot_general(w_buf[v:v + size, :], hid_buf[hid_slot], (((1,), (1,)), ((), ())),
                                preferred_element_type=jnp.float32) * INV_TEMP
            out[v:v + size, :] = z
            m = jnp.max(z, axis=0, keepdims=True)
            top = m if top is None else jnp.maximum(top, m)
        total = jnp.zeros_like(top)
        for v, size in spans:
            e = jnp.exp(out[v:v + size, :] - top)
            out[v:v + size, :] = e
            total = total + jnp.sum(e, axis=0, keepdims=True)
        return top, total

    for mb in range(2):
        first = mb * (depth + 1)

        def position(i, carry, mb=mb, first=first):
            slot = lax.rem(first + i, 2)
            load_hid(mb, i + 1, 1 - slot).start()
            load_hid(mb, i, slot).wait()
            g = mb * depth + i
            top, total = logits(slot, ex.at[g])
            loc_max[g] = top
            for h in range(halves):
                st_send[g * halves + h, 0:1, :] = top[:, h * LANES:(h + 1) * LANES]
                st_send[g * halves + h, 1:2, :] = total[:, h * LANES:(h + 1) * LANES]
            return carry

        lax.fori_loop(0, depth, position, 0)
        slot = (first + depth) % 2
        if mb == 0:
            load_hid(1, 0, 1 - slot).start()
        load_hid(mb, depth, slot).wait()
        top, total = logits(slot, eb.at[mb])
        loc_max[rounds + mb] = top
        for i in range(depth):
            for h in range(halves):
                d = (mb * depth + i) * halves + h
                st_send[d, 2:3, :] = top[:, h * LANES:(h + 1) * LANES]
                st_send[d, 3:4, :] = total[:, h * LANES:(h + 1) * LANES]

    def scatter(src, dst, sems):
        for step in steps:
            to = partner(step)
            pltpu.make_async_remote_copy(
                src_ref=src.at[to], dst_ref=dst.at[me], send_sem=sems.at[0], recv_sem=sems.at[1],
                device_id={'tp': to}, device_id_type=MESH).start()
        dst[me] = src[me]

    def spread(src, dst, sems):
        for step in steps:
            pltpu.make_async_remote_copy(
                src_ref=src, dst_ref=dst.at[me], send_sem=sems.at[2], recv_sem=sems.at[3],
                device_id={'tp': partner(step)}, device_id_type=MESH).start()
        dst[me] = src[...]

    scatter(st_send, st_recv, st_sem)
    lax.fori_loop(HEAD_ROUNDS, HEAD_ROUNDS + 2, head_round, 0)
    wait_tiles(st_recv, st_sem.at[1])
    for r in (0, 2):
        m = st_recv[:, r, :]
        top = jnp.max(m, axis=0, keepdims=True)
        total = jnp.sum(st_recv[:, r + 1, :] * jnp.exp(m - top), axis=0, keepdims=True)
        st_out[r:r + 1, :] = top
        st_out[r + 1:r + 2, :] = 1.0 / total
    spread(st_out, st_res, st_sem)
    lax.fori_loop(HEAD_ROUNDS + 2, depth, head_round, 0)
    load_q(1)
    wait_tiles(st_res, st_sem.at[3])

    for mb in range(2):
        for h in range(halves):
            d = mb * depth * halves + h
            lanes = slice(h * LANES, (h + 1) * LANES)
            f = jnp.exp(loc_max[rounds + mb][:, lanes] - st_res[d, 2:3, :]) * st_res[d, 3:4, :]
            eb[mb, :, lanes] = eb[mb, :, lanes] * f

    def process(g):
        block = recv.at[g, pl.ds(0, (n - 1) * SUBLANES)]
        pltpu.make_async_copy(block, block, recv_sem.at[g]).wait()
        for h in range(halves):
            lanes = slice(h * LANES, (h + 1) * LANES)
            d = g * halves + h
            f = jnp.exp(loc_max[g][:, lanes] - st_res[d, 0:1, :]) * st_res[d, 1:2, :]
            tok = tok_buf[g][:, lanes] - me * vocab

            def tile(v, size, sums):
                qt = recv[g, lanes, pl.ds(v, LANES)].T[:size]
                p = ex[g, pl.ds(v, size), lanes] * f
                x = jnp.maximum(p - qt, 0.0)
                ex[g, pl.ds(v, size), lanes] = x
                hit = lax.broadcasted_iota(jnp.int32, (size, LANES), 0) == tok - v
                zero = jnp.zeros_like(qt)
                parts = (x, jnp.where(hit, qt, zero), jnp.where(hit, p, zero))
                return tuple(s + jnp.sum(a, axis=0, keepdims=True) for s, a in zip(sums, parts))

            zero = jnp.zeros((1, LANES), jnp.float32)
            whole = vocab // LANES
            sums = lax.fori_loop(
                0, whole, lambda t, s: tile(pl.multiple_of(t * LANES, LANES), LANES, s), (zero, zero, zero))
            if vocab % LANES:
                sums = tile(whole * LANES, vocab % LANES, sums)
            for k in range(3):
                z_send[d, k:k + 1, :] = sums[k]

            @pl.when(me != d)
            def _():
                pltpu.make_async_remote_copy(
                    src_ref=z_send.at[d], dst_ref=z_recv.at[me], send_sem=z_sem.at[0], recv_sem=z_sem.at[1],
                    device_id={'tp': d}, device_id_type=MESH).start()

            @pl.when(me == d)
            def _():
                z_recv[me] = z_send[d]

    wait_q()

    def main_round(r, carry):
        wait_send(r - SLOTS)
        pack(r)
        send(r)
        process(r - SLOTS)
        return carry

    lax.fori_loop(depth, rounds, main_round, 0)

    def tail_round(g, carry):
        process(g)
        return carry

    lax.fori_loop(rounds - SLOTS, rounds, tail_round, 0)

    wait_tiles(z_recv, z_sem.at[1])
    sums = jnp.sum(z_recv[...], axis=0)
    z_out[0:1, :] = 1.0 / sums[0:1]
    z_out[1:2, :] = jnp.minimum(sums[2:3] / sums[1:2], 1.0)
    spread(z_out, z_res, z_sem)

    def drain(r, carry):
        wait_send(r)
        return carry

    lax.fori_loop(rounds - SLOTS, rounds, drain, 0)
    wait_tiles(st_send, st_sem.at[0])
    wait_tiles(st_res, st_sem.at[2])
    wait_tiles(z_send, z_sem.at[0])
    wait_tiles(z_res, z_sem.at[3])
    fin[...] = z_res[...]
    wait_tiles(z_res, z_sem.at[2])


def finish_kernel(depth, ex, eb, fin, res_one, res_two, bon_one, bon_two, acc_one, acc_two, exp_one, exp_two,
                  buf, sem, b_sem):
    ress, bons, accs, exps = (res_one, res_two), (bon_one, bon_two), (acc_one, acc_two), (exp_one, exp_two)
    halves = eb.shape[2] // LANES
    slots = buf.shape[0]
    for mb in range(2):
        pltpu.make_async_copy(eb.at[mb], bons[mb], b_sem.at[mb]).start()
    pending = []
    for mb in range(2):
        for i in range(depth):
            g = mb * depth + i
            if g >= slots:
                pending[g - slots].wait()
            for h in range(halves):
                lanes = slice(h * LANES, (h + 1) * LANES)
                buf[g % slots, :, lanes] = ex[g, :, lanes] * fin[g * halves + h, 0:1, :]
            copy = pltpu.make_async_copy(buf.at[g % slots], ress[mb].at[i], sem.at[g % slots])
            copy.start()
            pending.append(copy)
    for mb in range(2):
        for h in range(halves):
            lanes = slice(h * LANES, (h + 1) * LANES)
            prod = jnp.ones((1, LANES), jnp.float32)
            total = jnp.zeros((1, LANES), jnp.float32)
            for i in range(depth):
                a = fin[(mb * depth + i) * halves + h, 1:2, :]
                accs[mb][i:i + 1, lanes] = a
                prod = prod * a
                total = total + prod
            exps[mb][:, lanes] = total
    for copy in pending[-slots:]:
        copy.wait()
    for mb in range(2):
        pltpu.make_async_copy(eb.at[mb], bons[mb], b_sem.at[mb]).wait()


def verify_both(n, hid_one, q_one, tok_one, hid_two, q_two, tok_two, w_local):
    seqs, depth, whole_vocab = q_one.shape
    batch, vocab, hidden = hid_one.shape[0], w_local.shape[1], hid_one.shape[2]
    halves = batch // LANES
    rounds = 2 * depth
    width = pl.cdiv(vocab, LANES) * LANES
    assert seqs == SUBLANES and rounds * halves == n and batch == n * seqs
    f32 = jnp.float32
    vmem = pl.BlockSpec(memory_space=pltpu.VMEM)
    anys = pl.BlockSpec(memory_space=pl.ANY)
    tile = (n, SUBLANES, LANES)
    ex, eb, fin = pl.pallas_call(
        functools.partial(exchange_kernel, n),
        out_shape=(pltpu.VMEM((rounds, vocab, batch), f32), pltpu.VMEM((2, vocab, batch), f32), pltpu.VMEM(tile, f32)),
        in_specs=[anys, anys, anys, anys, vmem, vmem, anys],
        out_specs=(vmem, vmem, vmem),
        scratch_shapes=[
            pltpu.VMEM((vocab, hidden), w_local.dtype),
            pltpu.VMEM((2, batch, hidden), hid_one.dtype),
            pltpu.VMEM((whole_vocab // LANES + 1, seqs * depth, LANES), f32),
            pltpu.VMEM((SLOTS, n, SUBLANES, width), f32),
            pltpu.VMEM((rounds, batch, width), f32),
            pltpu.VMEM((rounds + 2, 1, batch), f32),
            pltpu.VMEM((rounds, 1, batch), jnp.int32),
            pltpu.VMEM(tile, f32), pltpu.VMEM(tile, f32), pltpu.VMEM(tile[1:], f32), pltpu.VMEM(tile, f32),
            pltpu.VMEM(tile, f32), pltpu.VMEM(tile, f32), pltpu.VMEM(tile[1:], f32), pltpu.VMEM(tile, f32),
            pltpu.SemaphoreType.DMA, pltpu.SemaphoreType.DMA, pltpu.SemaphoreType.DMA((2,)),
            pltpu.SemaphoreType.DMA((SLOTS,)), pltpu.SemaphoreType.DMA((rounds,)),
            pltpu.SemaphoreType.DMA((4,)), pltpu.SemaphoreType.DMA((4,)),
        ],
        compiler_params=pltpu.CompilerParams(collective_id=0, has_side_effects=True, vmem_limit_bytes=44 * 2 ** 20),
        name='exchange',
    )(jnp.swapaxes(hid_one, 0, 1), jnp.swapaxes(hid_two, 0, 1),
      q_one.reshape(seqs * depth, whole_vocab), q_two.reshape(seqs * depth, whole_vocab),
      tok_one.T, tok_two.T, w_local.T)

    shapes = [(depth, vocab, batch)] * 2 + [(vocab, batch)] * 2 + [(depth, batch)] * 2 + [(1, batch)] * 2
    outs = pl.pallas_call(
        functools.partial(finish_kernel, depth),
        out_shape=[jax.ShapeDtypeStruct(s, f32) for s in shapes],
        in_specs=[vmem] * 3,
        out_specs=[anys] * 4 + [vmem] * 4,
        scratch_shapes=[pltpu.VMEM((4, vocab, batch), f32), pltpu.SemaphoreType.DMA((4,)), pltpu.SemaphoreType.DMA((2,))],
        compiler_params=pltpu.CompilerParams(vmem_limit_bytes=12 * 2 ** 20),
        name='finish',
    )(ex, eb, fin)
    res, bon, acc, tot = outs[0:2], outs[2:4], outs[4:6], outs[6:8]
    result = ()
    for mb in range(2):
        result += (acc[mb].T, tot[mb].reshape(batch), jnp.transpose(res[mb], (2, 0, 1)), bon[mb].T)
    return result


def solution(mesh):
    row_spec = P('dp')
    q_spec = P(('dp', 'tp'))
    w_spec = P(None, 'tp')
    vocab_spec = P('dp', None, 'tp')
    bonus_spec = P('dp', 'tp')
    out_specs = (row_spec, row_spec, vocab_spec, bonus_spec) * 2
    in_specs = (row_spec, q_spec, row_spec, row_spec, q_spec, row_spec, w_spec)
    return jax.shard_map(functools.partial(verify_both, mesh.shape['tp']), mesh=mesh,
                         in_specs=in_specs, out_specs=out_specs, check_vma=False)
```

time: 1230 us -> 248 us (0.20); the launches traced: 1210 us -> 248 us
  local copies, waits for them, and re-layouts: 819 us -> 0 us
  Pallas kernels: 0 us -> 247 us
  blocking collectives: 236 us -> 0 us
  other arithmetic: 107 us -> 0 us
  matrix products: 29.9 us -> 0 us
  starting transfers between devices: 16.1 us -> 0 us
    unnamed x38 -> x0, local copies, waits for them, and re-layouts: 513 us -> none
    pallas_call x0 -> x2, Pallas kernels: none -> 247 us  [the longest x1 240 us: verify_both(): pl.pallas_call(functools.partial(exchange_kernel, n), out_shape=(pltpu.VM...]
    all_to_all x5 -> x0, local copies, waits for them, and re-layouts: 165 us -> none  [verify_local(): q_cols = lax.all_to_all(q_rows, 'tp', 2, 0, tiled=True)]
    gather x16 -> x0, local copies, waits for them, and re-layouts: 138 us -> none  [the longest x10 69.6 us: verify_local(): p_pick = jnp.take_along_axis(p_draft, tok_clip, axis=-1)[:, :, 0]]
    pmax x1 -> x0, blocking collectives: 129 us -> none  [verify_local(): row_max = lax.pmax(jnp.max(logits, axis=-1, keepdims=True), 'tp')]
    psum x2 -> x0, blocking collectives: 107 us -> none  [the longest x1 62.1 us: verify_local(): lax.psum(jnp.where(in_shard, jnp.stack([p_pick, q_pick]), 0.0), 'tp')]
    all_to_all x2 -> x0, other arithmetic: 49.6 us -> none  [verify_local(): q_cols = lax.all_to_all(q_rows, 'tp', 2, 0, tiled=True)]
    dot_general x2 -> x0, matrix products: 29.9 us -> none  [verify_local(): jnp.einsum('bgd,dv->bgv', hidden, w_local, preferred_element_type=jnp.flo...]
  transfers between devices with their start and end apart: 2 -> 0, of which waited for: 0 -> 0; matrix products, arithmetic and copies ran while one was open for 41% -> 0% of each run, Pallas kernels for 0% -> 0%
where the time goes in v1:
time: 248 us
  Pallas kernels  247 us (100%)
    pallas_call x1, Pallas kernels, verify_both(): pl.pallas_call(functools.partial(exchange_kernel, n), out_shape=(pltpu.VM...  240 us
    pallas_call x1, Pallas kernels, verify_both(): pl.pallas_call(functools.partial(finish_kernel, depth), out_shape=[jax.Sh...  7 us

profile of v1, /device:TPU:97, one launch (start us, length us, event | category | flops | bytes accessed | tf_op | source)
XLA Modules:
  0.0 247.5 jit_solution(4418351179195297261)
XLA Ops:
  0.6 239.9 %exchange.1 = (f32[16,1000,256]{2,1,0:T(8,128)S(1)}, f32[2,1000,256]{2,1,0:T(8,128)S(1)}, f32[32,8,128]{2,1,0:T(8,128)S(1)}) custom-call(bf16[9,256,2048]{2,1,0:T(8,128)(2,1)} %bitcast.15, bf16[9,256,2048]{2,1,0:T(8,128)(2,1)} %bitcast.16, f32[64,32000]{1,0:T(8,128)} %bitcast.17, f32[64,32000]{1,0:T(8,128)} %bitcast.18, s32[8,256]{1,0:T(8,128)} %bitcast.20, ...), custom_call_target="tpu_custom_call" | custom-call | tf_op jit(solution)/shard_map/exchange/pallas_call | solution.py:343
  240.5 7.0 %finish.1 = (f32[8,1000,256]{2,1,0:T(8,128)}, f32[8,1000,256]{2,1,0:T(8,128)}, f32[1000,256]{1,0:T(8,128)}, f32[1000,256]{1,0:T(8,128)}, f32[8,256]{1,0:T(8,128)...) custom-call(f32[16,1000,256]{2,1,0:T(8,128)S(1)} %get-tuple-element.19.ex, ...), custom_call_target="tpu_custom_call" | custom-call | tf_op jit(solution)/shard_map/finish/pallas_call | solution.py:369

commit v2 on v1

--- a/solution.py
+++ b/solution.py
@@ -14,45 +14,47 @@
 SLOTS = 8
 HEAD_ROUNDS = 4
 COL_TILE = 256
+LATE_ROUNDS = 2
+UNROLL = 7
+PACK_UNROLL = 4
 MESH = pl.DeviceIdType.MESH
 
 
-def partner_steps(n):
-    side = math.isqrt(n // 2)
-    groups = {}
-    for dy in range(side):
-        for dx in range(side):
-            hops = tuple(sorted((min(dy, side - dy), min(dx, side - dx)), reverse=True))
-            groups.setdefault(hops, []).append((dy, dx))
-    order = [(2, 2), (2, 1), (2, 0), (1, 0), (1, 1), (0, 0)]
-    order += [k for k in groups if k not in order]
-    steps = []
-    for key in order:
-        for dc in range(2):
-            for dy, dx in groups.get(key, []):
-                if (dy, dx, dc) != (0, 0, 0):
-                    steps.append((dy, dx, dc))
-    return steps
+def partner_steps(side):
+    one, back, half = 1, side - 1, side // 2
+    classes = [
+        [(half, one), (half, back), (one, half), (back, half)],
+        [(half, half)],
+        [(half, 0), (0, half)],
+        [(one, one), (back, back)],
+        [(one, back), (back, one)],
+        [(one, 0), (back, 0), (0, one), (0, back)],
+        [(0, 0)],
+    ]
+    assert sorted(d for c in classes for d in c) == [(x, y) for x in range(side) for y in range(side)]
+    return [(dx, dy, dc) for c in classes for dc in range(2) for dx, dy in c if (dx, dy, dc) != (0, 0, 0)]
 
 
 def exchange_kernel(n, hid_one, hid_two, q_one, q_two, tok_one, tok_two, w_hbm,
                     ex, eb, fin,
                     w_buf, hid_buf, q_buf, stage, recv, loc_max, tok_buf,
-                    st_send, st_recv, st_out, st_res, z_send, z_recv, z_out, z_res,
-                    q_sem, w_sem, hid_sem, send_sem, recv_sem, st_sem, z_sem):
+                    st_send, st_recv, st_out, st_res, z_send, z_recv, z_out, z_res, late_send, late_recv, guests,
+                    q_sem, w_sem, hid_sem, send_sem, recv_sem, st_sem, z_sem, late_sem):
     me = lax.axis_index('tp')
     depth, batch = tok_one.shape
     vocab = w_hbm.shape[0]
     halves = batch // LANES
     rounds = 2 * depth
+    early = (rounds - LATE_ROUNDS) * halves
     hids, qs, toks = (hid_one, hid_two), (q_one, q_two), (tok_one, tok_two)
     side = math.isqrt(n // 2)
     core, chip = lax.rem(me, 2), me // 2
     col, row = lax.rem(chip, side), chip // side
-    steps = partner_steps(n)
+    steps = partner_steps(side)
 
     def partner(step):
-        dy, dx, dc = step
+        dx, dy, dc = step
+        dy = dy + core * ((side - dy) % side - dy)
         return (lax.rem(row + dy, side) * side + lax.rem(col + dx, side)) * 2 + lax.rem(core + dc, 2)
 
     barrier = pltpu.get_barrier_semaphore()
@@ -80,18 +82,28 @@
     load_w = pltpu.make_async_copy(w_hbm, w_buf, w_sem)
     load_w.start()
     load_hid(0, 0, 0).start()
-    st_send[...] = jnp.zeros_like(st_send)
-    z_send[...] = jnp.zeros_like(z_send)
-    st_out[...] = jnp.zeros_like(st_out)
-    z_out[...] = jnp.zeros_like(z_out)
     for g in range(rounds):
         i = g % depth
         tok_buf[g] = toks[g // depth][i:i + 1, :]
     lane = lax.broadcasted_iota(jnp.int32, (SUBLANES, LANES), 1)
     tiles = pl.cdiv(vocab, LANES)
+    used = vocab - (tiles - 1) * LANES
+    gap = LANES - used
+    spread_pos = pl.cdiv(used, gap)
+    assert spread_pos < depth and gap % SUBLANES == 0
+
+    def narrow(r, action):
+        @pl.when(lax.rem(r, depth) == spread_pos)
+        def _():
+            action((tiles - 1) * LANES)
+
+        @pl.when(lax.rem(r, depth) != spread_pos)
+        def _():
+            action(tiles * LANES)
 
     def pack(r):
         i, slot = lax.rem(r, depth), lax.rem(r, SLOTS)
+        to_gap = lax.rem(used + depth * LANES - gap * i, LANES)
 
         def one(d, carry):
             start = d * vocab
@@ -100,26 +112,38 @@
             rolled = []
             for t in range(tiles + 1):
                 rolled.append(pltpu.roll(q_buf[base + t, pl.ds(i, SUBLANES, stride=depth), :], shift, 1))
-            for t in range(tiles):
+            for t in range(tiles - 1):
                 stage[slot, d, :, t * LANES:(t + 1) * LANES] = jnp.where(lane < LANES - off, rolled[t], rolled[t + 1])
+            last = jnp.where(lane < LANES - off, rolled[tiles - 1], rolled[tiles])
+            guest = [pltpu.roll(q_buf[base + t, pl.ds(spread_pos, SUBLANES, stride=depth), :], shift, 1)
+                     for t in (tiles - 1, tiles)]
+            guest = pltpu.roll(jnp.where(lane < LANES - off, guest[0], guest[1]), to_gap, 1)
+            stage[slot, d, :, (tiles - 1) * LANES:] = jnp.where(lane < used, last, guest)
             return carry
 
-        lax.fori_loop(0, n, one, 0)
+        lax.fori_loop(0, n, one, 0, unroll=PACK_UNROLL)
 
     def send(r):
         slot = lax.rem(r, SLOTS)
         mine = pl.ds(pl.multiple_of(me * SUBLANES, SUBLANES), SUBLANES)
-        for step in steps:
-            to = partner(step)
-            pltpu.make_async_remote_copy(
-                src_ref=stage.at[slot, to], dst_ref=recv.at[r, mine],
-                send_sem=send_sem.at[slot], recv_sem=recv_sem.at[r],
-                device_id={'tp': to}, device_id_type=MESH).start()
+
+        def start(width):
+            for step in steps:
+                to = partner(step)
+                pltpu.make_async_remote_copy(
+                    src_ref=stage.at[slot, to, :, pl.ds(0, width)], dst_ref=recv.at[r, mine, pl.ds(0, width)],
+                    send_sem=send_sem.at[slot], recv_sem=recv_sem.at[r],
+                    device_id={'tp': to}, device_id_type=MESH).start()
+
+        narrow(r, start)
         recv[r, mine, :] = stage[slot, me]
 
     def wait_send(r):
-        block = stage.at[lax.rem(r, SLOTS), pl.ds(0, n - 1)]
-        pltpu.make_async_copy(block, block, send_sem.at[lax.rem(r, SLOTS)]).wait()
+        def wait(width):
+            block = stage.at[lax.rem(r, SLOTS), pl.ds(0, n - 1), :, pl.ds(0, width)]
+            pltpu.make_async_copy(block, block, send_sem.at[lax.rem(r, SLOTS)]).wait()
+
+        narrow(r, wait)
 
     def wait_tiles(ref, sem):
         block = ref.at[pl.ds(0, n - 1)]
@@ -219,33 +243,53 @@
             f = jnp.exp(loc_max[rounds + mb][:, lanes] - st_res[d, 2:3, :]) * st_res[d, 3:4, :]
             eb[mb, :, lanes] = eb[mb, :, lanes] * f
 
-    def process(g):
-        block = recv.at[g, pl.ds(0, (n - 1) * SUBLANES)]
-        pltpu.make_async_copy(block, block, recv_sem.at[g]).wait()
+    def process(g, late=False):
+        def wait(width):
+            block = recv.at[g, pl.ds(0, (n - 1) * SUBLANES), pl.ds(0, width)]
+            pltpu.make_async_copy(block, block, recv_sem.at[g]).wait()
+
+        narrow(g, wait)
+        i = lax.rem(g, depth)
+        scales, picks, sums = [], [], []
         for h in range(halves):
             lanes = slice(h * LANES, (h + 1) * LANES)
             d = g * halves + h
-            f = jnp.exp(loc_max[g][:, lanes] - st_res[d, 0:1, :]) * st_res[d, 1:2, :]
-            tok = tok_buf[g][:, lanes] - me * vocab
-
-            def tile(v, size, sums):
-                qt = recv[g, lanes, pl.ds(v, LANES)].T[:size]
-                p = ex[g, pl.ds(v, size), lanes] * f
+            scales.append(jnp.exp(loc_max[g][:, lanes] - st_res[d, 0:1, :]) * st_res[d, 1:2, :])
+            picks.append(tok_buf[g][:, lanes] - me * vocab)
+            sums += [jnp.zeros((SUBLANES, LANES), jnp.float32)] * 3
+
+        def tile(v, size, sums, last=False):
+            line = lax.broadcasted_iota(jnp.int32, (size, LANES), 0)
+            after = []
+            for h in range(halves):
+                lanes = slice(h * LANES, (h + 1) * LANES)
+                qt = recv[g, lanes, pl.ds(v, LANES)].T
+                if last:
+                    guests[pl.ds(pl.multiple_of(i * gap, SUBLANES), gap), lanes] = qt[size:]
+                    qt = jnp.where(i == spread_pos, guests[0:size, lanes], qt[:size])
+                p = ex[g, pl.ds(v, size), lanes] * scales[h]
                 x = jnp.maximum(p - qt, 0.0)
                 ex[g, pl.ds(v, size), lanes] = x
-                hit = lax.broadcasted_iota(jnp.int32, (size, LANES), 0) == tok - v
-                zero = jnp.zeros_like(qt)
-                parts = (x, jnp.where(hit, qt, zero), jnp.where(hit, p, zero))
-                return tuple(s + jnp.sum(a, axis=0, keepdims=True) for s, a in zip(sums, parts))
-
-            zero = jnp.zeros((1, LANES), jnp.float32)
-            whole = vocab // LANES
-            sums = lax.fori_loop(
-                0, whole, lambda t, s: tile(pl.multiple_of(t * LANES, LANES), LANES, s), (zero, zero, zero))
-            if vocab % LANES:
-                sums = tile(whole * LANES, vocab % LANES, sums)
-            for k in range(3):
-                z_send[d, k:k + 1, :] = sums[k]
+                hit = line == picks[h] - v
+                for k, part in enumerate((x, jnp.where(hit, qt, 0.0), jnp.where(hit, p, 0.0))):
+                    fold = jnp.sum(part.reshape(size // SUBLANES, SUBLANES, LANES), axis=0)
+                    after.append(sums[3 * h + k] + fold)
+            return tuple(after)
+
+        sums = lax.fori_loop(
+            0, tiles - 1, lambda t, s: tile(pl.multiple_of(t * LANES, LANES), LANES, s), tuple(sums), unroll=UNROLL)
+        sums = tile((tiles - 1) * LANES, used, sums, last=True)
+        for h in range(halves):
+            d = g * halves + h
+            total, q_pick, p_pick = (jnp.sum(a, axis=0, keepdims=True) for a in sums[3 * h:3 * h + 3])
+            found = (picks[h] >= 0) & (picks[h] < vocab)
+            accept = jnp.where(found, jnp.minimum(p_pick / q_pick, 1.0), 0.0)
+            if late:
+                late_send[2 * (d - early)] = total
+                late_send[2 * (d - early) + 1] = accept
+                continue
+            z_send[d, 0:1, :] = total
+            z_send[d, 1:2, :] = accept
 
             @pl.when(me != d)
             def _():
@@ -272,13 +316,20 @@
         process(g)
         return carry
 
-    lax.fori_loop(rounds - SLOTS, rounds, tail_round, 0)
-
-    wait_tiles(z_recv, z_sem.at[1])
-    sums = jnp.sum(z_recv[...], axis=0)
-    z_out[0:1, :] = 1.0 / sums[0:1]
-    z_out[1:2, :] = jnp.minimum(sums[2:3] / sums[1:2], 1.0)
-    spread(z_out, z_res, z_sem)
+    lax.fori_loop(rounds - SLOTS, rounds - LATE_ROUNDS, tail_round, 0)
+    for g in range(rounds - LATE_ROUNDS, rounds - 1):
+        process(g, late=True)
+
+    @pl.when(me < early)
+    def _():
+        wait_tiles(z_recv, z_sem.at[1])
+        sums = jnp.sum(z_recv[...], axis=0)
+        z_out[0:1, :] = 1.0 / sums[0:1]
+        z_out[1:2, :] = sums[1:2]
+        spread(z_out, z_res, z_sem)
+
+    process(rounds - 1, late=True)
+    spread(late_send, late_recv, late_sem)
 
     def drain(r, carry):
         wait_send(r)
@@ -287,10 +338,29 @@
     lax.fori_loop(rounds - SLOTS, rounds, drain, 0)
     wait_tiles(st_send, st_sem.at[0])
     wait_tiles(st_res, st_sem.at[2])
-    wait_tiles(z_send, z_sem.at[0])
-    wait_tiles(z_res, z_sem.at[3])
-    fin[...] = z_res[...]
-    wait_tiles(z_res, z_sem.at[2])
+
+    def wait_some(ref, count, sem):
+        block = ref.at[pl.ds(0, count)]
+        pltpu.make_async_copy(block, block, sem).wait()
+
+    @pl.when(me < early)
+    def _():
+        wait_some(z_send, early - 1, z_sem.at[0])
+        wait_tiles(z_res, z_sem.at[2])
+        wait_some(z_res, early - 1, z_sem.at[3])
+
+    @pl.when(me >= early)
+    def _():
+        wait_some(z_send, early, z_sem.at[0])
+        wait_some(z_res, early, z_sem.at[3])
+
+    fin[0:early] = z_res[0:early]
+    wait_tiles(late_recv, late_sem.at[3])
+    late = jnp.sum(late_recv[...], axis=0)
+    for k in range(n - early):
+        fin[early + k, 0:1, :] = 1.0 / late[2 * k]
+        fin[early + k, 1:2, :] = late[2 * k + 1]
+    wait_tiles(late_recv, late_sem.at[2])
 
 
 def finish_kernel(depth, ex, eb, fin, res_one, res_two, bon_one, bon_two, acc_one, acc_two, exp_one, exp_two,
@@ -339,10 +409,10 @@
     f32 = jnp.float32
     vmem = pl.BlockSpec(memory_space=pltpu.VMEM)
     anys = pl.BlockSpec(memory_space=pl.ANY)
-    tile = (n, SUBLANES, LANES)
+    late = (2 * LATE_ROUNDS * halves, 1, LANES)
     ex, eb, fin = pl.pallas_call(
         functools.partial(exchange_kernel, n),
-        out_shape=(pltpu.VMEM((rounds, vocab, batch), f32), pltpu.VMEM((2, vocab, batch), f32), pltpu.VMEM(tile, f32)),
+        out_shape=(pltpu.VMEM((rounds, vocab, batch), f32), pltpu.VMEM((2, vocab, batch), f32), pltpu.VMEM((n, 2, LANES), f32)),
         in_specs=[anys, anys, anys, anys, vmem, vmem, anys],
         out_specs=(vmem, vmem, vmem),
         scratch_shapes=[
@@ -353,11 +423,12 @@
             pltpu.VMEM((rounds, batch, width), f32),
             pltpu.VMEM((rounds + 2, 1, batch), f32),
             pltpu.VMEM((rounds, 1, batch), jnp.int32),
-            pltpu.VMEM(tile, f32), pltpu.VMEM(tile, f32), pltpu.VMEM(tile[1:], f32), pltpu.VMEM(tile, f32),
-            pltpu.VMEM(tile, f32), pltpu.VMEM(tile, f32), pltpu.VMEM(tile[1:], f32), pltpu.VMEM(tile, f32),
+            pltpu.VMEM((n, 4, LANES), f32), pltpu.VMEM((n, 4, LANES), f32), pltpu.VMEM((4, LANES), f32), pltpu.VMEM((n, 4, LANES), f32),
+            pltpu.VMEM((n, 2, LANES), f32), pltpu.VMEM((n, 2, LANES), f32), pltpu.VMEM((2, LANES), f32), pltpu.VMEM((n, 2, LANES), f32),
+            pltpu.VMEM(late, f32), pltpu.VMEM((n,) + late, f32), pltpu.VMEM((depth * (width - vocab), batch), f32),
             pltpu.SemaphoreType.DMA, pltpu.SemaphoreType.DMA, pltpu.SemaphoreType.DMA((2,)),
             pltpu.SemaphoreType.DMA((SLOTS,)), pltpu.SemaphoreType.DMA((rounds,)),
-            pltpu.SemaphoreType.DMA((4,)), pltpu.SemaphoreType.DMA((4,)),
+            pltpu.SemaphoreType.DMA((4,)), pltpu.SemaphoreType.DMA((4,)), pltpu.SemaphoreType.DMA((4,)),
         ],
         compiler_params=pltpu.CompilerParams(collective_id=0, has_side_effects=True, vmem_limit_bytes=44 * 2 ** 20),
         name='exchange',

time: 248 us -> 220 us (0.89)
  Pallas kernels: 247 us -> 219 us
    pallas_call x1, Pallas kernels: 240 us -> 212 us  [verify_both(): pl.pallas_call(functools.partial(exchange_kernel, n), out_shape=(pltpu.VM...]
where the time goes in v2:
time: 220 us; the launch traced here: 219 us
  Pallas kernels  219 us (100%)
    pallas_call x1, Pallas kernels, verify_both(): pl.pallas_call(functools.partial(exchange_kernel, n), out_shape=(pltpu.VM...  212 us
    pallas_call x1, Pallas kernels, verify_both(): pl.pallas_call(functools.partial(finish_kernel, depth), out_shape=[jax.Sh...  7 us

profile of v2, /device:TPU:97, one launch (start us, length us, event | category | flops | bytes accessed | tf_op | source)
XLA Modules:
  0.0 219.4 jit_solution(16135621826568909524)
XLA Ops:
  0.6 211.6 %exchange.1 = (f32[16,1000,256]{2,1,0:T(8,128)S(1)}, f32[2,1000,256]{2,1,0:T(8,128)S(1)}, f32[32,2,128]{2,1,0:T(2,128)S(1)}) custom-call(bf16[9,256,2048]{2,1,0:T(8,128)(2,1)} %bitcast.15, bf16[9,256,2048]{2,1,0:T(8,128)(2,1)} %bitcast.16, f32[64,32000]{1,0:T(8,128)} %bitcast.17, f32[64,32000]{1,0:T(8,128)} %bitcast.18, s32[8,256]{1,0:T(8,128)} %bitcast.20, ...), custom_call_target="tpu_custom_call" | custom-call | tf_op jit(solution)/shard_map/exchange/pallas_call | solution.py:413
  212.2 7.0 %finish.1 = (f32[8,1000,256]{2,1,0:T(8,128)}, f32[8,1000,256]{2,1,0:T(8,128)}, f32[1000,256]{1,0:T(8,128)}, f32[1000,256]{1,0:T(8,128)}, f32[8,256]{1,0:T(8,128)...) custom-call(f32[16,1000,256]{2,1,0:T(8,128)S(1)} %get-tuple-element.19.ex, ...), custom_call_target="tpu_custom_call" | custom-call | tf_op jit(solution)/shard_map/finish/pallas_call | solution.py:440

commit v3 on v2

--- a/solution.py
+++ b/solution.py
@@ -17,6 +17,7 @@
 LATE_ROUNDS = 2
 UNROLL = 7
 PACK_UNROLL = 4
+CHUNKS = 4
 MESH = pl.DeviceIdType.MESH
 
 
@@ -61,19 +62,24 @@
     for step in steps:
         pl.semaphore_signal(barrier, inc=1, device_id={'tp': partner(step)}, device_id_type=MESH)
 
-    q_tiles = q_one.shape[1] // LANES
+    seqs, q_tiles = q_one.shape[0], q_one.shape[1] // depth
+    pitch = (q_tiles + 1) * depth
+    tiles = pl.cdiv(vocab, LANES)
+    share = n // CHUNKS
+    ends = [min(q_tiles, ((k + 1) * share - 1) * vocab // LANES + tiles + 1) for k in range(CHUNKS)]
+    chunks = list(zip([0] + ends[:-1], ends))
 
     def load_q(mb):
-        def one(t, carry):
-            cols = pl.ds(pl.multiple_of(t * LANES, LANES), LANES)
-            pltpu.make_async_copy(qs[mb].at[:, cols], q_buf.at[t], q_sem).start()
-            return carry
-
-        lax.fori_loop(0, q_tiles, one, 0)
-
-    def wait_q():
-        block = q_buf.at[pl.ds(0, q_tiles)]
-        pltpu.make_async_copy(block, block, q_sem).wait()
+        for k, (low, high) in enumerate(chunks):
+            for b in range(seqs):
+                pltpu.make_async_copy(
+                    qs[mb].at[b, pl.ds(low * depth, (high - low) * depth)],
+                    q_buf.at[pl.ds(b * pitch + low * depth, (high - low) * depth)], q_sem.at[k]).start()
+
+    def wait_q(k):
+        low, high = chunks[k]
+        block = q_buf.at[pl.ds(0, seqs * (high - low) * depth)]
+        pltpu.make_async_copy(block, block, q_sem.at[k]).wait()
 
     def load_hid(mb, i, slot):
         return pltpu.make_async_copy(hids[mb].at[i], hid_buf.at[slot], hid_sem.at[slot])
@@ -86,7 +92,6 @@
         i = g % depth
         tok_buf[g] = toks[g // depth][i:i + 1, :]
     lane = lax.broadcasted_iota(jnp.int32, (SUBLANES, LANES), 1)
-    tiles = pl.cdiv(vocab, LANES)
     used = vocab - (tiles - 1) * LANES
     gap = LANES - used
     spread_pos = pl.cdiv(used, gap)
@@ -101,7 +106,7 @@
         def _():
             action(tiles * LANES)
 
-    def pack(r):
+    def pack(r, first=0, count=n):
         i, slot = lax.rem(r, depth), lax.rem(r, SLOTS)
         to_gap = lax.rem(used + depth * LANES - gap * i, LANES)
 
@@ -111,17 +116,17 @@
             shift = lax.rem(LANES - off, LANES)
             rolled = []
             for t in range(tiles + 1):
-                rolled.append(pltpu.roll(q_buf[base + t, pl.ds(i, SUBLANES, stride=depth), :], shift, 1))
+                rolled.append(pltpu.roll(q_buf[pl.ds((base + t) * depth + i, seqs, stride=pitch), :], shift, 1))
             for t in range(tiles - 1):
                 stage[slot, d, :, t * LANES:(t + 1) * LANES] = jnp.where(lane < LANES - off, rolled[t], rolled[t + 1])
             last = jnp.where(lane < LANES - off, rolled[tiles - 1], rolled[tiles])
-            guest = [pltpu.roll(q_buf[base + t, pl.ds(spread_pos, SUBLANES, stride=depth), :], shift, 1)
+            guest = [pltpu.roll(q_buf[pl.ds((base + t) * depth + spread_pos, seqs, stride=pitch), :], shift, 1)
                      for t in (tiles - 1, tiles)]
             guest = pltpu.roll(jnp.where(lane < LANES - off, guest[0], guest[1]), to_gap, 1)
             stage[slot, d, :, (tiles - 1) * LANES:] = jnp.where(lane < used, last, guest)
             return carry
 
-        lax.fori_loop(0, n, one, 0, unroll=PACK_UNROLL)
+        lax.fori_loop(first, first + count, one, 0, unroll=PACK_UNROLL)
 
     def send(r):
         slot = lax.rem(r, SLOTS)
@@ -149,8 +154,9 @@
         block = ref.at[pl.ds(0, n - 1)]
         pltpu.make_async_copy(block, block, sem).wait()
 
-    wait_q()
-    pack(0)
+    for k in range(CHUNKS):
+        wait_q(k)
+        pack(0, k * share, share)
     pl.semaphore_wait(barrier, n - 1)
     send(0)
 
@@ -301,7 +307,8 @@
             def _():
                 z_recv[me] = z_send[d]
 
-    wait_q()
+    for k in range(CHUNKS):
+        wait_q(k)
 
     def main_round(r, carry):
         wait_send(r - SLOTS)
@@ -405,11 +412,16 @@
     halves = batch // LANES
     rounds = 2 * depth
     width = pl.cdiv(vocab, LANES) * LANES
-    assert seqs == SUBLANES and rounds * halves == n and batch == n * seqs
+    assert seqs == SUBLANES and depth == SUBLANES and rounds * halves == n and batch == n * seqs
     f32 = jnp.float32
     vmem = pl.BlockSpec(memory_space=pltpu.VMEM)
     anys = pl.BlockSpec(memory_space=pl.ANY)
     late = (2 * LATE_ROUNDS * halves, 1, LANES)
+
+    def by_tile(q):
+        q = q.reshape(seqs, depth, whole_vocab // LANES, LANES)
+        return jnp.swapaxes(q, 1, 2).reshape(seqs, whole_vocab // LANES * depth, LANES)
+
     ex, eb, fin = pl.pallas_call(
         functools.partial(exchange_kernel, n),
         out_shape=(pltpu.VMEM((rounds, vocab, batch), f32), pltpu.VMEM((2, vocab, batch), f32), pltpu.VMEM((n, 2, LANES), f32)),
@@ -418,7 +430,7 @@
         scratch_shapes=[
             pltpu.VMEM((vocab, hidden), w_local.dtype),
             pltpu.VMEM((2, batch, hidden), hid_one.dtype),
-            pltpu.VMEM((whole_vocab // LANES + 1, seqs * depth, LANES), f32),
+            pltpu.VMEM((seqs * (whole_vocab // LANES + 1) * depth, LANES), f32),
             pltpu.VMEM((SLOTS, n, SUBLANES, width), f32),
             pltpu.VMEM((rounds, batch, width), f32),
             pltpu.VMEM((rounds + 2, 1, batch), f32),
@@ -426,14 +438,14 @@
             pltpu.VMEM((n, 4, LANES), f32), pltpu.VMEM((n, 4, LANES), f32), pltpu.VMEM((4, LANES), f32), pltpu.VMEM((n, 4, LANES), f32),
             pltpu.VMEM((n, 2, LANES), f32), pltpu.VMEM((n, 2, LANES), f32), pltpu.VMEM((2, LANES), f32), pltpu.VMEM((n, 2, LANES), f32),
             pltpu.VMEM(late, f32), pltpu.VMEM((n,) + late, f32), pltpu.VMEM((depth * (width - vocab), batch), f32),
-            pltpu.SemaphoreType.DMA, pltpu.SemaphoreType.DMA, pltpu.SemaphoreType.DMA((2,)),
+            pltpu.SemaphoreType.DMA((CHUNKS,)), pltpu.SemaphoreType.DMA, pltpu.SemaphoreType.DMA((2,)),
             pltpu.SemaphoreType.DMA((SLOTS,)), pltpu.SemaphoreType.DMA((rounds,)),
             pltpu.SemaphoreType.DMA((4,)), pltpu.SemaphoreType.DMA((4,)), pltpu.SemaphoreType.DMA((4,)),
         ],
         compiler_params=pltpu.CompilerParams(collective_id=0, has_side_effects=True, vmem_limit_bytes=44 * 2 ** 20),
         name='exchange',
     )(jnp.swapaxes(hid_one, 0, 1), jnp.swapaxes(hid_two, 0, 1),
-      q_one.reshape(seqs * depth, whole_vocab), q_two.reshape(seqs * depth, whole_vocab),
+      by_tile(q_one), by_tile(q_two),
       tok_one.T, tok_two.T, w_local.T)
 
     shapes = [(depth, vocab, batch)] * 2 + [(vocab, batch)] * 2 + [(depth, batch)] * 2 + [(1, batch)] * 2

time: 220 us -> 217 us (0.986)
  Pallas kernels: 219 us -> 216 us
    pallas_call x1, Pallas kernels: 212 us -> 209 us  [verify_both(): pl.pallas_call(functools.partial(exchange_kernel, n), out_shape=(pltpu.VM...]
where the time goes in v3:
time: 217 us
  Pallas kernels  216 us (100%)
    pallas_call x1, Pallas kernels, verify_both(): pl.pallas_call(functools.partial(exchange_kernel, n), out_shape=(pltpu.VM...  209 us
    pallas_call x1, Pallas kernels, verify_both(): pl.pallas_call(functools.partial(finish_kernel, depth), out_shape=[jax.Sh...  7 us

profile of v3, /device:TPU:97, one launch (start us, length us, event | category | flops | bytes accessed | tf_op | source)
XLA Modules:
  0.0 216.9 jit_solution(14208245568355493253)
XLA Ops:
  0.6 209.1 %exchange.1 = (f32[16,1000,256]{2,1,0:T(8,128)S(1)}, f32[2,1000,256]{2,1,0:T(8,128)S(1)}, f32[32,2,128]{2,1,0:T(2,128)S(1)}) custom-call(bf16[9,256,2048]{2,1,0:T(8,128)(2,1)} %bitcast.23, bf16[9,256,2048]{2,1,0:T(8,128)(2,1)} %bitcast.24, f32[8,2000,128]{2,1,0:T(8,128)} %bitcast.25, f32[8,2000,128]{2,1,0:T(8,128)} %bitcast.26, s32[8,256]{1,0:T(8,128)} %bitcast.28, ...), custom_call_target="tpu_custom_call" | custom-call | tf_op jit(solution)/shard_map/exchange/pallas_call | solution.py:425
  209.8 7.0 %finish.1 = (f32[8,1000,256]{2,1,0:T(8,128)}, f32[8,1000,256]{2,1,0:T(8,128)}, f32[1000,256]{1,0:T(8,128)}, f32[1000,256]{1,0:T(8,128)}, f32[8,256]{1,0:T(8,128)...) custom-call(f32[16,1000,256]{2,1,0:T(8,128)S(1)} %get-tuple-element.19.ex, ...), custom_call_target="tpu_custom_call" | custom-call | tf_op jit(solution)/shard_map/finish/pallas_call | solution.py:452
